TPU v7x, 32 devices: a 4x2x2 block of a 4x4x8 slice. The times are simulated.
32 devices in a mesh: dp: 4 (over y, z), tp: 8 (over x, core).
Axes of the slice: x: 4, y: 2, z: 2, core: 2. Of those that a mesh axis runs over, the one named last changes fastest.
The devices are a block of a 4x4x8 slice.
Arguments:
- x: bfloat16 [12288, 4096], P('dp'), parts along dimension 0
- lens: int32 [8], P('dp'), parts along dimension 0
- g1: bfloat16 [4096], replicated
- g2: bfloat16 [4096], replicated
- wq: bfloat16 [4096, 4096], P(None, 'tp')
- wk: bfloat16 [4096, 1024], replicated
- wv: bfloat16 [4096, 1024], replicated
- wo: bfloat16 [4096, 4096], P('tp')
- wg: bfloat16 [4096, 14336], P(None, 'tp')
- wu: bfloat16 [4096, 14336], P(None, 'tp')
- wd: bfloat16 [14336, 4096], P('tp')
Outputs:
- output 1: bfloat16 [12288, 4096], P('dp'), parts along dimension 0
- output 2: bfloat16 [8, 3072, 8, 128], P('dp', None, 'tp'), parts along dimension 0
- output 3: bfloat16 [8, 3072, 8, 128], P('dp', None, 'tp'), parts along dimension 0
There are 4 independent parts. A program takes and returns all parts, laid end to end along the dimension named above; an argument that names none is the same for every part.
All inputs are finite; a program needn't handle non-finite values.
Results may differ from a plain program's by a relative error of at most 0.0155253.
Values are sent between devices in bfloat16 or wider.
A program may use at most 768 MiB of HBM per device.

v0:
```python
import math
import jax
import jax.numpy as jnp
from jax import lax
from jax.sharding import PartitionSpec as P

HEAD = 128
EPS = 1e-5
BASE = 500000.0


def _mm(a, b):
    return jnp.dot(a, b, preferred_element_type=jnp.float32)


def _rms(x, g):
    xf = x.astype(jnp.float32)
    ms = jnp.mean(xf * xf, axis=-1, keepdims=True)
    return (xf * lax.rsqrt(ms + EPS) * g.astype(jnp.float32)).astype(jnp.bfloat16)


def _rope(x, pos):
    inv = BASE ** (-jnp.arange(0, HEAD, 2, dtype=jnp.float32) / HEAD)
    ang = pos.astype(jnp.float32)[:, None] * inv[None, :]
    c = jnp.cos(ang)[:, None, :]
    s = jnp.sin(ang)[:, None, :]
    x1 = x[..., : HEAD // 2]
    x2 = x[..., HEAD // 2 :]
    return jnp.concatenate([x1 * c - x2 * s, x2 * c + x1 * s], axis=-1)


def _add(x, p):
    return (x.astype(jnp.float32) + p.astype(jnp.float32)).astype(jnp.bfloat16)


def _swiglu(gate, up):
    gate = gate.astype(jnp.bfloat16).astype(jnp.float32)
    up = up.astype(jnp.bfloat16).astype(jnp.float32)
    return (jax.nn.silu(gate) * up).astype(jnp.bfloat16)


def _attend(q, k, v, qrow, seg):
    n = q.shape[0]
    qb = math.gcd(n, 256)
    cols = jnp.arange(k.shape[0])

    def block(args):
        qq, rr = args
        s = jnp.einsum('qgrd,kgd->grqk', qq, k, preferred_element_type=jnp.float32) * HEAD ** -0.5
        mask = (cols[None, :] <= rr[:, None]) & (seg[None, :] == seg[rr][:, None])
        s = jnp.where(mask, s, -jnp.inf)
        pr = jax.nn.softmax(s, axis=-1).astype(jnp.bfloat16)
        return jnp.einsum('grqk,kgd->qgrd', pr, v, preferred_element_type=jnp.float32).astype(jnp.bfloat16)

    o = lax.map(block, (q.reshape(n // qb, qb, *q.shape[1:]), qrow.reshape(n // qb, qb)))
    return o.reshape(n, -1)


def _cache(k, l1):
    t = k.shape[0]
    rows = jnp.arange(t)
    z = jnp.zeros((), k.dtype)
    c1 = jnp.where((rows < l1)[:, None, None], k, z)
    c2 = jnp.where((rows < t - l1)[:, None, None], jnp.take(k, (rows + l1) % t, axis=0), z)
    return jnp.stack([c1, c2])


def solution(mesh):
    tp = mesh.shape['tp']

    def layer(x, lens, g1, g2, wq, wk, wv, wo, wg, wu, wd):
        n = x.shape[0]
        t = lax.axis_index('tp')
        g = wk.shape[1] // HEAD
        kvr = max(g, tp)
        kvl = kvr // tp
        hl = wq.shape[1] // HEAD
        l1 = lens[0]
        rows = jnp.arange(n)
        seg = (rows >= l1).astype(jnp.int32)
        pos = jnp.where(seg == 1, rows - l1, rows)
        c0 = (t * kvl * g // kvr) * HEAD
        wk_l = lax.dynamic_slice_in_dim(wk, c0, kvl * HEAD, axis=1)
        wv_l = lax.dynamic_slice_in_dim(wv, c0, kvl * HEAD, axis=1)
        a = _rms(x, g1)
        q = _rope(_mm(a, wq).reshape(n, hl, HEAD), pos).astype(jnp.bfloat16)
        k = _rope(_mm(a, wk_l).reshape(n, kvl, HEAD), pos).astype(jnp.bfloat16)
        v = _mm(a, wv_l).astype(jnp.bfloat16).reshape(n, kvl, HEAD)
        o = _attend(q.reshape(n, kvl, hl // kvl, HEAD), k, v, rows, seg)
        p = lax.psum(_mm(o, wo).astype(jnp.bfloat16), 'tp')
        h = _add(x, p)
        b = _rms(h, g2)
        u = _swiglu(_mm(b, wg), _mm(b, wu))
        r = lax.psum(_mm(u, wd).astype(jnp.bfloat16), 'tp')
        y = _add(h, r)
        return y, _cache(k, l1), _cache(v, l1)

    row = P('dp', None)
    cache = P('dp', None, 'tp', None)
    return jax.shard_map(
        layer, mesh=mesh,
        in_specs=(row, P('dp'), P(), P(), P(None, 'tp'), P(), P(), P('tp', None),
                  P(None, 'tp'), P(None, 'tp'), P('tp', None)),
        out_specs=(row, cache, cache), check_vma=False)
```

profile of v0, /device:TPU:81, one launch (start us, length us, event | category | flops | bytes accessed | tf_op | source)
XLA Modules:
  0.0 1068.5 jit_solution(16345638565280161970)
XLA Ops:
  7.3 10.3 fusion.24
  18.4 23.0 %fusion.26 = bf16[3072,4096]{1,0:T(8,128)(2,1)} fusion(bf16[3072,4096]{1,0:T(8,128)(2,1)} %param.15, f32[4096]{0:T(1024)S(1)} %convert_element_type.113, f32[3072]{0:T(1024)S(1)} %add_rsqrt_fusion.1), kind=kLoop, calls=%fused_computation.38 | loop fusion | flops 50331648 | bytes 50360320 | tf_op jit(solution)/shard_map/convert_element_type | solution.py:19
  44.2 13.5 %convolution_bitcast_fusion = f32[3072,1,128]{0,2,1:T(8,128)S(1)} fusion(bf16[3072,4096]{1,0:T(8,128)(2,1)} %fusion.26, bf16[4096,1024]{1,0:T(8,128)(2,1)} %param.20, s32[]{:T(128)S(6)} %select_n.78), kind=kOutput, calls=%fused_computation.56 | convolution fusion | flops 3221225472 | bytes 27787268 | tf_op jit(solution)/shard_map/dot_general | solution.py:13
  62.4 13.5 %convolution_convert_fusion.4 = bf16[3072,128]{0,1:T(8,128)(2,1)S(1)} fusion(bf16[3072,4096]{1,0:T(8,128)(2,1)} %fusion.26, bf16[4096,1024]{1,0:T(8,128)(2,1)} %param.21, s32[]{:T(128)S(6)} %select_n.78), kind=kOutput, calls=%fused_computation.57 | convolution fusion | flops 3221618688 | bytes 27000836 | tf_op jit(solution)/shard_map/dot_general | solution.py:13
  77.0 19.9 %fusion.63 = f32[3072,512]{0,1:T(8,128)} fusion(bf16[3072,4096]{1,0:T(8,128)(2,1)} %fusion.26, bf16[4096,512]{1,0:T(8,128)(2,1)} %param.19), kind=kOutput, calls=%fused_computation.107 | convolution fusion | flops 12884901888 | bytes 35651584 | tf_op jit(solution)/shard_map/dot_general | solution.py:13
  97.0 5.5 subtract_convert_fusion
  105.3 3.9 concatenate.43
  109.3 4.1 pad_maximum_fusion
  113.4 7.4 copy.24
  120.8 182.3 %while.11 = (s32[]{:T(128)}, bf16[12,256,1,4,128]{4,3,1,0,2:T(4,128)(2,1)}, s32[12,256]{1,0:T(8,128)S(1)}, bf16[12,256,1,4,128]{4,1,3,2,0:T(8,128)(2,1)}, bf16[3...) while((s32[]{:T(128)}, ...), condition=%wide.region_4.5_spmd.clone, body=%wide.region_1.4_spmd.clone.sunk | while | flops 1650857728 | bytes 46721144 | solution.py:55
  123.5 3.5 fusion.90
  127.1 3.7 fusion.91
  130.8 4.4 fusion.92
  142.2 3.7 fusion.91
  145.9 4.4 fusion.92
  153.9 3.5 fusion.90
  157.4 3.7 fusion.91
  161.1 4.4 fusion.92
  169.1 3.5 fusion.90
  172.6 3.7 fusion.91
  176.3 4.4 fusion.92
  187.8 3.7 fusion.91
  191.5 4.4 fusion.92
  202.9 3.7 fusion.91
  206.6 4.4 fusion.92
  218.1 3.7 fusion.91
  221.8 4.4 fusion.92
  233.3 3.7 fusion.91
  237.0 4.4 fusion.92
  248.5 3.7 fusion.91
  252.2 4.4 fusion.92
  263.6 3.7 fusion.91
  267.4 4.4 fusion.92
  278.8 3.7 fusion.91
  282.5 4.4 fusion.92
  290.5 3.5 fusion.90
  294.0 3.7 fusion.91
  297.7 4.4 fusion.92
  303.1 21.1 %convolution_convert_fusion = bf16[3072,4096]{1,0:T(8,128)(2,1)} fusion(bf16[512,4096]{1,0:T(8,128)(2,1)} %param.22, bf16[384,8,4,128]{3,2,1,0:T(4,128)(2,1)} %bitcast.37), kind=kOutput, calls=%fused_computation.46 | convolution fusion | flops 12897484800 | bytes 32505856 | tf_op jit(solution)/shard_map/dot_general | solution.py:13
  324.9 258.8 %all-reduce.3.cloned.1.call-done = bf16[3072,4096]{1,0:T(8,128)(2,1)} async-done(((bf16[3072,4096]{1,0:T(8,128)(2,1)}), bf16[3072,4096]{1,0:T(8,128)(2,1)}) %all-reduce.3.cloned.1.call-update) | async-done | bytes 25165840 | tf_op jit(solution)/shard_map/psum | solution.py:90
  583.7 29.4 %fusion.28 = (f32[3072]{0:T(1024)S(1)}, bf16[3072,4096]{1,0:T(8,128)(2,1)}) fusion(bf16[3072,4096]{1,0:T(8,128)(2,1)} %all-reduce.3.cloned.1.call-done, bf16[3072,4096]{1,0:T(8,128)(2,1)} %param.15), kind=kLoop, calls=%fused_computation.40 | loop fusion | flops 88077312 | bytes 75509760 | tf_op jit(solution)/shard_map/reduce_sum | solution.py:18
  613.1 53.8 %convolution_convert_fusion.3 = bf16[3072,1792]{1,0:T(8,128)(2,1)S(1)} fusion(bf16[4096,1792]{1,0:T(8,128)(2,1)} %param.23, bf16[3072,4096]{1,0:T(8,128)(2,1)} %get-tuple-element.102, f32[4096]{0:T(1024)S(1)} %convert_element_type.121, f32[3072]{0:T(1024)S(1)} %add_rsqrt_fusion), kind=kOutput, calls=%fused_computation.54 | convolution fusion | flops 45152993280 | bytes 50884608 | tf_op jit(solution)/shard_map/dot_general | solution.py:13
  666.9 56.3 %fusion.36 = bf16[3072,1792]{1,0:T(8,128)(2,1)} fusion(bf16[3072,1792]{1,0:T(8,128)(2,1)S(1)} %convolution_convert_fusion.3, bf16[4096,1792]{1,0:T(8,128)(2,1)} %param.24, bf16[3072,4096]{1,0:T(8,128)(2,1)} %get-tuple-element.102, f32[4096]{0:T(1024)S(1)} %convert_element_type.121, f32[3072]{0:T(1024)S(1)} %add_rsqrt_fusion), kind=kOutput, calls=%fused_computation.52 | convolution fusion | flops 45197033472 | bytes 61894656 | tf_op jit(solution)/shard_map/dot_general | solution.py:13
  723.3 53.9 %convolution_convert_fusion.1 = bf16[3072,4096]{1,0:T(8,128)(2,1)} fusion(bf16[3072,1792]{1,0:T(8,128)(2,1)} %fusion.36, bf16[1792,4096]{1,0:T(8,128)(2,1)} %param.25), kind=kOutput, calls=%fused_computation.47 | convolution fusion | flops 45109739520 | bytes 50855936 | tf_op jit(solution)/shard_map/dot_general | solution.py:13
  780.2 11.6 %gather_fusion.1 = bf16[3072,128]{1,0:T(8,128)(2,1)} fusion(bf16[3072,128]{1,0:T(8,128)(2,1)S(1)} %copy.28, s32[3072]{0:T(1024)S(1)} %copy-done.7), kind=kCustom, calls=%fused_computation.1.clone | custom fusion | bytes 1585152 | tf_op jit(solution)/shard_map/jit(_take)/gather | solution.py:64
  793.2 11.6 %gather_fusion.2 = bf16[3072,128]{1,0:T(8,128)(2,1)} fusion(bf16[3072,128]{1,0:T(8,128)(2,1)S(1)} %copy.30, s32[3072]{0:T(1024)S(1)} %copy-done.7), kind=kCustom, calls=%fused_computation.2.clone | custom fusion | bytes 1585152 | tf_op jit(solution)/shard_map/jit(_take)/gather | solution.py:64
  810.2 222.5 %all-reduce.5.cloned.1.call-done = bf16[3072,4096]{1,0:T(8,128)(2,1)} async-done(((bf16[3072,4096]{1,0:T(8,128)(2,1)}), bf16[3072,4096]{1,0:T(8,128)(2,1)}) %all-reduce.5.cloned.1.call-update) | async-done | bytes 25165840 | tf_op jit(solution)/shard_map/psum | solution.py:94
  1032.7 28.5 %fusion.31 = bf16[3072,4096]{1,0:T(8,128)(2,1)} fusion(bf16[3072,4096]{1,0:T(8,128)(2,1)} %get-tuple-element.102, bf16[3072,4096]{1,0:T(8,128)(2,1)} %all-reduce.5.cloned.1.call-done), kind=kLoop, calls=%fused_computation.43 | loop fusion | flops 50331648 | bytes 75497472 | tf_op jit(solution)/shard_map/convert_element_type | solution.py:33
  (157 shorter events, 92.5 us)
Async XLA Ops:
  7.2 576.5 %all-reduce.3.cloned.1.call-start = ((), (), s32[]{:S(2)}) async-start(), calls=%async_computation | async-start | bytes 50331648 | tf_op jit(solution)/shard_map/psum | solution.py:90
  7.3 10.4 copy-start.10
  7.3 10.4 copy-start.8
  60.9 1.1 copy-start.2
  60.9 1.1 copy-start.4
  75.9 21.1 %copy-start = (bf16[3072,128]{0,1:T(8,128)(2,1)}, bf16[3072,128]{0,1:T(8,128)(2,1)S(1)}, u32[]{:S(2)}) copy-start(bf16[3072,128]{0,1:T(8,128)(2,1)S(1)} %convolution_convert_fusion.4) | copy-start | bytes 2359300
  123.5 7.2 copy-start.6
  138.7 7.2 copy-start.6
  153.9 7.2 copy-start.6
  169.1 7.2 copy-start.6
  184.2 7.2 copy-start.6
  199.4 7.2 copy-start.6
  214.6 7.2 copy-start.6
  229.7 7.2 copy-start.6
  244.9 7.2 copy-start.6
  260.1 7.2 copy-start.6
  275.3 7.2 copy-start.6
  290.5 7.2 copy-start.6
  324.2 0.7 copy-start.11
  324.3 708.4 %all-reduce.5.cloned.1.call-start = ((), (), s32[]{:S(2)}) async-start(), calls=%async_computation.1 | async-start | bytes 50331648 | tf_op jit(solution)/shard_map/psum | solution.py:94
  777.1 1.1 copy-start.1
  777.1 3.0 copy-start.7
  778.3 27.9 %copy-start.9 = (s32[2]{0:T(128)S(1)}, s32[2]{0:T(128)}, u32[]{:S(2)}) copy-start(s32[2]{0:T(128)} %param.16) | copy-start | bytes 28
  778.3 28.0 %copy-start.3 = (bf16[3072,1,64]{0,2,1:T(8,128)(2,1)S(1)}, bf16[3072,1,64]{0,2,1:T(8,128)(2,1)}, u32[]{:S(2)}) copy-start(bf16[3072,1,64]{0,2,1:T(8,128)(2,1)} %copy-done.2) | copy-start | bytes 1179652
  778.3 28.0 %copy-start.5 = (bf16[3072,1,64]{0,2,1:T(8,128)(2,1)S(1)}, bf16[3072,1,64]{0,2,1:T(8,128)(2,1)}, u32[]{:S(2)}) copy-start(bf16[3072,1,64]{0,2,1:T(8,128)(2,1)} %copy-done.4) | copy-start | bytes 1179652
Sparse Core Ops, SparseCore 0:
  324.4 259.2 all-reduce.2
  777.3 255.3 all-reduce.4
where the time goes:
time: 1080 us; the launch traced here: 1070 us
  waiting for transfers between devices  481 us (45%)
  matrix products  327 us (30%)
  other arithmetic  164 us (15%)
  local copies, waits for them, and re-layouts  80.1 us (7%)
  between operations  14.8 us (1%)
    psum x1, waiting for transfers between devices, layer(): p = lax.psum(_mm(o, wo).astype(jnp.bfloat16), 'tp')  259 us
    dot_general x7, matrix products, _mm(): return jnp.dot(a, b, preferred_element_type=jnp.float32)  232 us
    psum x1, waiting for transfers between devices, layer(): r = lax.psum(_mm(u, wd).astype(jnp.bfloat16), 'tp')  223 us
    dot_general x12, matrix products, block(): jnp.einsum('grqk,kgd->qgrd', pr, v, preferred_element_type=jnp.float32)  53.4 us
    reduce_sum x12, other arithmetic, block(): pr = jax.nn.softmax(s, axis=-1).astype(jnp.bfloat16)  44.3 us
    dot_general x12, matrix products, block(): jnp.einsum('qgrd,kgd->grqk', qq, k, preferred_element_type=jnp.float32)  42.1 us
    reduce_sum x2, other arithmetic, _rms(): ms = jnp.mean(xf * xf, axis=-1, keepdims=True)  39.7 us
    convert_element_type x1, other arithmetic, _add(): return (x.astype(jnp.float32) + p.astype(jnp.float32)).astype(jnp.bfloat16)  28.5 us
  transfers between devices with their start and end apart: 2, of which 2 were waited for; matrix products, arithmetic and copies ran while one was open for 3% of the time, Pallas kernels for 0%

commit v1 on v0

v1 whole, which is shorter than its diff:
```python
import functools

import jax
import jax.numpy as jnp
from jax import lax
from jax.experimental import pallas as pl
from jax.experimental.pallas import tpu as pltpu
from jax.sharding import PartitionSpec as P

HEAD = 128
EPS = 1e-5
BASE = 500000.0
VMEM_LIMIT = 67000000
F32 = jnp.float32
BF16 = jnp.bfloat16
ANY = pl.BlockSpec(memory_space=pl.ANY)


def _rows_per_chunk(n):
    return 384 if n % 384 == 0 else 128


def _dot(a, b):
    return jnp.dot(a, b, preferred_element_type=F32)


def _cols(i, size):
    return pl.ds(pl.multiple_of(i * size, size), size)


def _rows(i, size):
    return pl.ds(pl.multiple_of(i * size, size), size)


def _norm_chunk(m, x_ref, g, a_ref):
    def body(k, _):
        r = _rows(k, 16)
        xf = x_ref[r, :].astype(F32)
        ms = jnp.mean(xf * xf, axis=-1, keepdims=True)
        a_ref[r, :] = (xf * lax.rsqrt(ms + EPS) * g).astype(BF16)
        return 0

    lax.fori_loop(0, m // 16, body, 0)


def _rope(z, cos, sin):
    return z * cos + pltpu.roll(z, HEAD // 2, 1) * sin


def _project_chunk(i, m, a_ref, wq_ref, wkv_ref, cos_ref, sin_ref, q_ref, k_ref, v_ref):
    a = a_ref[...]
    cos, sin = cos_ref[...], sin_ref[...]
    kv = _dot(a, wkv_ref[...])
    r = _rows(i, m)
    k_ref[r, :] = _rope(kv[:, :HEAD], cos, sin).astype(BF16)
    v_ref[r, :] = kv[:, HEAD:].astype(BF16)
    q = _dot(a, wq_ref[...])
    for h in range(q_ref.shape[0]):
        q_ref[h] = _rope(q[:, h * HEAD:(h + 1) * HEAD], cos, sin).astype(BF16)


def _attend_chunk(i, m, l1, q_ref, k_ref, v_ref, s_ref, o_ref):
    rows = i * m + lax.broadcasted_iota(jnp.int32, (m, 1), 0)
    first = jnp.where(rows >= l1, l1, 0)
    scale = HEAD ** -0.5 * 1.4426950408889634

    def head(h, _):
        q = q_ref[h]

        def score(b, top):
            s = lax.dot_general(q, k_ref[_rows(b, m), :], (((1,), (1,)), ((), ())), preferred_element_type=F32)
            cols = b * m + lax.broadcasted_iota(jnp.int32, (1, m), 1)
            s = jnp.where((cols <= rows) & (cols >= first), s, -jnp.inf)
            s_ref[b] = s
            return jnp.maximum(top, jnp.max(s, axis=1, keepdims=True))

        top = lax.fori_loop(0, i + 1, score, jnp.full((m, 1), -jnp.inf, F32))

        def expo(b, total):
            e = jnp.exp2((s_ref[b] - top) * scale)
            s_ref[b] = e
            return total + jnp.sum(e, axis=1, keepdims=True)

        total = lax.fori_loop(0, i + 1, expo, jnp.zeros((m, 1), F32))
        inv = 1.0 / total

        def value(b, acc):
            return acc + _dot((s_ref[b] * inv).astype(BF16), v_ref[_rows(b, m), :])

        acc = lax.fori_loop(0, i + 1, value, jnp.zeros((m, HEAD), F32))
        o_ref[:, _cols(h, HEAD)] = acc.astype(BF16)
        return 0

    lax.fori_loop(0, q_ref.shape[0], head, 0)


def _attention_kernel(m, l1_ref, x_ref, g_ref, cos_ref, sin_ref, wq_ref, wkv_ref, o_ref, kc_ref, vc_ref,
                      a_buf, q_buf, k_buf, v_buf, s_buf):
    i = pl.program_id(0)
    _norm_chunk(m, x_ref, g_ref[...].astype(F32), a_buf)
    _project_chunk(i, m, a_buf, wq_ref, wkv_ref, cos_ref, sin_ref, q_buf, k_buf, v_buf)
    kc_ref[...] = k_buf[_rows(i, m), :]
    vc_ref[...] = v_buf[_rows(i, m), :]
    _attend_chunk(i, m, l1_ref[0], q_buf, k_buf, v_buf, s_buf, o_ref)


def _attention(x, lens, g1, cos, sin, wq, wkv):
    n, d = x.shape
    m = _rows_per_chunk(n)
    hq = wq.shape[1]
    full = lambda s: pl.BlockSpec(s, lambda i: (0, 0), pipeline_mode=pl.Buffered(buffer_count=1))
    row = lambda c: pl.BlockSpec((m, c), lambda i: (i, 0))
    return pl.pallas_call(
        functools.partial(_attention_kernel, m),
        grid=(n // m,),
        out_shape=(jax.ShapeDtypeStruct((n, hq), BF16), jax.ShapeDtypeStruct((n, HEAD), BF16),
                   jax.ShapeDtypeStruct((n, HEAD), BF16)),
        in_specs=[pl.BlockSpec(memory_space=pltpu.SMEM), row(d), full((1, d)), row(HEAD), row(HEAD),
                  full((d, hq)), full((d, 2 * HEAD))],
        out_specs=(row(hq), row(HEAD), row(HEAD)),
        scratch_shapes=[pltpu.VMEM((m, d), BF16), pltpu.VMEM((hq // HEAD, m, HEAD), BF16),
                        pltpu.VMEM((n, HEAD), BF16), pltpu.VMEM((n, HEAD), BF16),
                        pltpu.VMEM((n // m, m, m), F32)],
        compiler_params=pltpu.CompilerParams(vmem_limit_bytes=VMEM_LIMIT, dimension_semantics=("arbitrary",)),
        name="attention",
    )(lens, x, g1, cos, sin, wq, wkv)


class _Stream:
    def __init__(self, m, part, got, r1l, r1r, r2l, r2r, mine, whole, sems, finish):
        self.m, self.r = m, m // 8
        self.part, self.got, self.mine, self.whole = part, got, mine, whole
        self.r1l, self.r1r, self.r2l, self.r2r = r1l, r1r, r2l, r2r
        self.sems, self.finish = sems, finish
        self.h = part.shape[1] // 2
        t = lax.axis_index("tp")
        x, c = t // 2, t % 2
        self.x, self.c = x, c
        self.xr, self.xo, self.xl = (x + 1) % 4, (x + 2) % 4, (x + 3) % 4
        self.right, self.left = self.xr * 2 + c, self.xl * 2 + c
        self.twin = x * 2 + 1 - c
        self.lo, self.hi = pl.ds(0, self.h), pl.ds(self.h, self.h)

    def send(self, src, dst, k, slot, to):
        return pltpu.make_async_remote_copy(
            src_ref=src, dst_ref=dst, send_sem=self.sems.at[0, slot, k], recv_sem=self.sems.at[1, slot, k],
            device_id={"tp": to}, device_id_type=pl.DeviceIdType.MESH)

    def block(self, chip):
        return pl.ds(pl.multiple_of(chip * self.r, 16), self.r)

    def pair(self, i):
        s = i % 2
        theirs = pl.ds(pl.multiple_of((1 - self.c) * 4 * self.r, 16), 4 * self.r)
        return self.send(self.part.at[theirs, :], self.got.at[s], 0, s, self.twin)

    def first(self, i):
        s = i % 2
        got = self.got.at[s]
        return (
            self.send(got.at[self.block(self.xo), self.lo], self.r1l.at[s, :, self.lo], 1, s, self.right),
            self.send(got.at[self.block(self.xo), self.hi], self.r1r.at[s, :, self.hi], 2, s, self.left),
            self.send(got.at[self.block(self.xr), self.hi], self.r1l.at[s, :, self.hi], 3, s, self.right),
            self.send(got.at[self.block(self.xl), self.lo], self.r1r.at[s, :, self.lo], 4, s, self.left),
        )

    def second(self, i):
        s = i % 2
        got = self.got.at[s]
        return (
            self.send(got.at[self.block(self.xr), self.lo], self.r2l.at[s], 5, s, self.right),
            self.send(got.at[self.block(self.xl), self.hi], self.r2r.at[s], 6, s, self.left),
        )

    def place(self, i, chip):
        return pl.ds(pl.multiple_of(i * self.m + self.c * 4 * self.r + chip * self.r, 16), self.r)

    def own(self, i):
        s = i % 2
        mine, here = self.mine.at[s], self.whole.at[self.place(i, self.x), :]
        return (
            self.send(mine, here, 7, s, self.right),
            self.send(mine, here, 8, s, self.left),
            self.send(mine, here, 9, s, self.twin),
        )

    def keep(self, i):
        s = i % 2
        return pltpu.make_async_copy(self.mine.at[s], self.whole.at[self.place(i, self.x), :], self.sems.at[0, s, 15])

    def onward(self, i):
        s = i % 2
        a, b = self.whole.at[self.place(i, self.xl), self.lo], self.whole.at[self.place(i, self.xr), self.hi]
        return self.send(a, a, 10, s, self.right), self.send(b, b, 11, s, self.left)

    def across(self, i):
        s = i % 2
        a, b = self.whole.at[self.place(i, self.xl), :], self.whole.at[self.place(i, self.xr), :]
        return self.send(a, a, 12, s, self.twin), self.send(b, b, 13, s, self.twin)

    def last(self, i):
        s = i % 2
        a = self.whole.at[self.place(i, self.xo), :]
        return self.send(a, a, 14, s, self.twin)


    def s0(self, i):
        self.pair(i).start()

    def s1(self, i):
        self.pair(i).wait()
        s, r = i % 2, self.r
        base = self.c * 4 * r

        def add(k, _):
            a = _rows(k, 16)
            b = pl.ds(pl.multiple_of(base + k * 16, 16), 16)
            self.got[s, a, :] = (self.got[s, a, :].astype(F32) + self.part[b, :].astype(F32)).astype(BF16)
            return 0

        lax.fori_loop(0, 4 * r // 16, add, 0)
        for copy in self.first(i):
            copy.start()

    def s2(self, i):
        s, r = i % 2, self.r
        copies = self.first(i)
        for copy in copies:
            copy.wait_send()
        copies[0].wait_recv()
        copies[1].wait_recv()

        def add(k, _):
            a = _rows(k, 16)
            for chip, cols, new in ((self.xr, self.lo, self.r1l), (self.xl, self.hi, self.r1r)):
                b = pl.ds(pl.multiple_of(chip * r + k * 16, 16), 16)
                self.got[s, b, cols] = (self.got[s, b, cols].astype(F32) + new[s, a, cols].astype(F32)).astype(BF16)
            return 0

        lax.fori_loop(0, r // 16, add, 0)
        for copy in self.second(i):
            copy.start()

    def s3(self, i):
        s, r = i % 2, self.r
        copies = self.first(i)
        copies[2].wait_recv()
        copies[3].wait_recv()
        for copy in self.second(i):
            copy.wait()

        def add(k, _):
            a = _rows(k, 16)
            b = pl.ds(pl.multiple_of(self.x * r + k * 16, 16), 16)
            got = self.got[s, b, :].astype(F32)
            lo = got[:, :self.h] + self.r2l[s, a, :].astype(F32) + self.r1r[s, a, self.lo].astype(F32)
            hi = got[:, self.h:] + self.r1l[s, a, self.hi].astype(F32) + self.r2r[s, a, :].astype(F32)
            total = jnp.concatenate([lo, hi], axis=1).astype(BF16)
            self.mine[s, a, :] = self.finish(i, a, total)
            return 0

        lax.fori_loop(0, r // 16, add, 0)
        for copy in self.own(i):
            copy.start()
        self.keep(i).start()

    def s4(self, i):
        copies = self.own(i)
        for copy in copies:
            copy.wait_send()
        copies[0].wait_recv()
        copies[1].wait_recv()
        for copy in self.onward(i):
            copy.start()
        for copy in self.across(i):
            copy.start()

    def s5(self, i):
        for copy in self.onward(i):
            copy.wait()
        self.last(i).start()

    def s6(self, i):
        self.own(i)[2].wait_recv()
        for copy in self.across(i):
            copy.wait()
        self.last(i).wait()
        self.keep(i).wait()


def _layer_kernel(m, o_hbm, x_hbm, g_ref, wo_hbm, wg_hbm, wu_hbm, wd_hbm, y_hbm, b_hbm,
                  wo_buf, o_buf, x_buf, h_buf, b_buf, u_buf, wgu_buf, wd_buf,
                  p_part, p_got, p_r1l, p_r1r, p_r2l, p_r2r, p_mine,
                  r_part, r_got, r_r1l, r_r1r, r_r2l, r_r2r, r_mine,
                  p_sems, r_sems, sems, wgu_sems, wd_sems):
    n, d = x_hbm.shape
    f = wg_hbm.shape[1]
    ft, dt = wgu_buf.shape[2] // 2, wd_buf.shape[2]
    nf, nd, nc = f // ft, d // dt, n // m
    r = m // 8

    def finish_p(i, a, total):
        xf = x_buf[a, :].astype(F32) + total.astype(F32)
        h = xf.astype(BF16)
        h_buf[i, a, :] = h
        hf = h.astype(F32)
        ms = jnp.mean(hf * hf, axis=-1, keepdims=True)
        return (hf * lax.rsqrt(ms + EPS) * g_ref[...].astype(F32)).astype(BF16)

    def finish_r(i, a, total):
        return (h_buf[i, a, :].astype(F32) + total.astype(F32)).astype(BF16)

    ps = _Stream(m, p_part, p_got, p_r1l, p_r1r, p_r2l, p_r2r, p_mine, b_hbm, p_sems, finish_p)
    rs = _Stream(m, r_part, r_got, r_r1l, r_r1r, r_r2l, r_r2r, r_mine, y_hbm, r_sems, finish_r)

    barrier = pltpu.get_barrier_semaphore()
    for to in (ps.right, ps.left, ps.twin):
        pl.semaphore_signal(barrier, inc=1, device_id={"tp": to}, device_id_type=pl.DeviceIdType.MESH)
    pl.semaphore_wait(barrier, 3)

    def wgu(k, s):
        c = _cols(k, ft)
        return (pltpu.make_async_copy(wg_hbm.at[:, c], wgu_buf.at[s, :, pl.ds(0, ft)], wgu_sems.at[s, 0]),
                pltpu.make_async_copy(wu_hbm.at[:, c], wgu_buf.at[s, :, pl.ds(ft, ft)], wgu_sems.at[s, 1]))

    def wd(k, s):
        return pltpu.make_async_copy(wd_hbm.at[:, _cols(k, dt)], wd_buf.at[s], wd_sems.at[s])

    def load_o(i):
        return pltpu.make_async_copy(o_hbm.at[_rows(i, m), :], o_buf, sems.at[0])

    def load_x(i):
        return pltpu.make_async_copy(x_hbm.at[ps.place(i, ps.x), :], x_buf, sems.at[1])

    def load_b(i):
        return pltpu.make_async_copy(b_hbm.at[_rows(i, m), :], b_buf, sems.at[2])

    load_wo = pltpu.make_async_copy(wo_hbm, wo_buf, sems.at[3])
    load_o(0).start()
    load_wo.start()
    for k in range(2):
        for copy in wgu(k % nf, k):
            copy.start()
        wd(k % nd, k).start()

    def gate_up(i, lo, hi):
        def tile(k, _):
            at = i * nf + k
            s = at % 2
            for copy in wgu(k, s):
                copy.wait()
            z = _dot(b_buf[...], wgu_buf[s])
            gate = z[:, :ft].astype(BF16).astype(F32)
            up = z[:, ft:].astype(BF16).astype(F32)
            u_buf[:, _cols(k, ft)] = (gate * (1.0 / (1.0 + jnp.exp(-gate))) * up).astype(BF16)

            @pl.when(at + 2 < nc * nf)
            def _():
                for copy in wgu((k + 2) % nf, s):
                    copy.start()
            return 0

        lax.fori_loop(lo, hi, tile, 0)

    def down(i, lo, hi):
        def tile(k, _):
            at = i * nd + k
            s = at % 2
            wd(k, s).wait()
            r_part[:, _cols(k, dt)] = _dot(u_buf[...], wd_buf[s]).astype(BF16)

            @pl.when(at + 2 < nc * nd)
            def _():
                wd((k + 2) % nd, s).start()
            return 0

        lax.fori_loop(lo, hi, tile, 0)

    def out_proj(i):
        load_o(i).wait()

        @pl.when(i == 0)
        def _():
            load_wo.wait()

        def tile(k, _):
            p_part[:, _cols(k, dt)] = _dot(o_buf[...], wo_buf[:, _cols(k, dt)]).astype(BF16)
            return 0

        lax.fori_loop(0, nd, tile, 0)

        @pl.when(i + 1 < nc)
        def _():
            load_o(i + 1).start()

    def step(j, _):
        def at(delay):
            return lambda body: pl.when((j >= delay) & (j < nc + delay))(lambda: body(j - delay))

        at(4)(rs.s4)
        at(3)(rs.s1)
        at(0)(out_proj)
        at(1)(ps.s3)
        at(0)(ps.s0)

        @at(2)
        def _(i):
            ps.s6(i)
            load_b(i).start()
            load_b(i).wait()
            gate_up(i, 0, (nf + 1) // 2)

        at(4)(rs.s5)
        at(3)(rs.s2)
        at(2)(lambda i: gate_up(i, (nf + 1) // 2, nf))
        at(1)(ps.s4)
        at(0)(ps.s1)
        at(2)(lambda i: down(i, 0, nd // 2))
        at(4)(rs.s6)
        at(3)(rs.s3)
        at(2)(lambda i: down(i, nd // 2, nd))
        at(1)(ps.s5)

        @at(0)
        def _(i):
            load_x(i).start()
            ps.s2(i)
            load_x(i).wait()

        at(2)(rs.s0)
        return 0

    lax.fori_loop(0, nc + 5, step, 0)


def _layer_sums(o, x, g2, wo, wg, wu, wd):
    n, d = x.shape
    m = _rows_per_chunk(n)
    r, h, hq, f = m // 8, d // 2, o.shape[1], wg.shape[1]
    ft, dt = 256, 512
    stream = [pltpu.VMEM((m, d), BF16), pltpu.VMEM((2, 4 * r, d), BF16),
              pltpu.VMEM((2, r, d), BF16), pltpu.VMEM((2, r, d), BF16),
              pltpu.VMEM((2, r, h), BF16), pltpu.VMEM((2, r, h), BF16), pltpu.VMEM((2, r, d), BF16)]
    return pl.pallas_call(
        functools.partial(_layer_kernel, m),
        out_shape=(jax.ShapeDtypeStruct((n, d), BF16), jax.ShapeDtypeStruct((n, d), BF16)),
        in_specs=[ANY, ANY, pl.BlockSpec(memory_space=pltpu.VMEM), ANY, ANY, ANY, ANY],
        out_specs=(ANY, ANY),
        scratch_shapes=[
            pltpu.VMEM((hq, d), BF16), pltpu.VMEM((m, hq), BF16), pltpu.VMEM((r, d), BF16),
            pltpu.VMEM((n // m, r, d), BF16), pltpu.VMEM((m, d), BF16), pltpu.VMEM((m, f), BF16),
            pltpu.VMEM((2, d, 2 * ft), BF16), pltpu.VMEM((2, f, dt), BF16),
            *stream, *stream,
            pltpu.SemaphoreType.DMA((2, 2, 16)), pltpu.SemaphoreType.DMA((2, 2, 16)),
            pltpu.SemaphoreType.DMA((4,)), pltpu.SemaphoreType.DMA((2, 2)), pltpu.SemaphoreType.DMA((2,)),
        ],
        compiler_params=pltpu.CompilerParams(collective_id=0, has_side_effects=True, vmem_limit_bytes=VMEM_LIMIT),
        name="layer_sums",
    )(o, x, g2, wo, wg, wu, wd)


def _cache_kernel(m, l1_ref, k_ref, v_ref, ck_ref, cv_ref, k_buf, v_buf):
    i = pl.program_id(0)
    n = k_ref.shape[0]
    l1 = l1_ref[0]

    @pl.when(i == 0)
    def _():
        for src, buf in ((k_ref, k_buf), (v_ref, v_buf)):
            buf[pl.ds(0, n), :] = src[...].astype(F32)
            buf[pl.ds(n, m), :] = jnp.zeros((m, HEAD), F32)

    rows = i * m + lax.broadcasted_iota(jnp.int32, (m, 1), 0)
    start = jnp.minimum(l1 + i * m, n)
    for buf, out in ((k_buf, ck_ref), (v_buf, cv_ref)):
        out[0] = jnp.where(rows < l1, buf[_rows(i, m), :], 0.0).astype(BF16)
        out[1] = jnp.where(rows < n - l1, buf[pl.ds(start, m), :], 0.0).astype(BF16)


def _caches(lens, k, v):
    n = k.shape[0]
    m = _rows_per_chunk(n)
    whole = pl.BlockSpec((n, HEAD), lambda i: (0, 0))
    out = pl.BlockSpec((2, m, HEAD), lambda i: (0, i, 0))
    return pl.pallas_call(
        functools.partial(_cache_kernel, m),
        grid=(n // m,),
        out_shape=(jax.ShapeDtypeStruct((2, n, HEAD), BF16),) * 2,
        in_specs=[pl.BlockSpec(memory_space=pltpu.SMEM), whole, whole],
        out_specs=(out, out),
        scratch_shapes=[pltpu.VMEM((n + m, HEAD), F32), pltpu.VMEM((n + m, HEAD), F32)],
        compiler_params=pltpu.CompilerParams(dimension_semantics=("arbitrary",)),
        name="caches",
    )(lens, k, v)


def solution(mesh):
    assert mesh.shape["tp"] == 8

    def layer(x, lens, g1, g2, wq, wk, wv, wo, wg, wu, wd):
        n, d = x.shape
        t = lax.axis_index("tp")
        l1 = lens[0]
        rows = jnp.arange(n)
        pos = jnp.where(rows >= l1, rows - l1, rows)
        inv = BASE ** (-jnp.arange(0, HEAD, 2, dtype=F32) / HEAD)
        ang = pos.astype(F32)[:, None] * inv[None, :]
        c, s = jnp.cos(ang), jnp.sin(ang)
        cos = jnp.concatenate([c, c], axis=1)
        sin = jnp.concatenate([-s, s], axis=1)
        wkv = jnp.concatenate([lax.dynamic_slice_in_dim(w, t * HEAD, HEAD, axis=1) for w in (wk, wv)], axis=1)
        o, k, v = _attention(x, lens, g1[None], cos, sin, wq, wkv)
        y, _ = _layer_sums(o, x, g2[None], wo, wg, wu, wd)
        ck, cv = _caches(lens, k, v)
        return y, ck[:, :, None, :], cv[:, :, None, :]

    row = P("dp", None)
    cache = P("dp", None, "tp", None)
    return jax.shard_map(
        layer, mesh=mesh,
        in_specs=(row, P("dp"), P(), P(), P(None, "tp"), P(), P(), P("tp", None),
                  P(None, "tp"), P(None, "tp"), P("tp", None)),
        out_specs=(row, cache, cache), check_vma=False)
```

time: 1080 us -> 662 us (0.61)
  Pallas kernels: 0 us -> 625 us
  waiting for transfers between devices: 481 us -> 0 us
  matrix products: 327 us -> 0 us
  other arithmetic: 164 us -> 10.6 us
  local copies, waits for them, and re-layouts: 80.1 us -> 24.5 us
  between operations: 14.8 us -> 0.66 us
    pallas_call x0 -> x3, Pallas kernels: none -> 625 us  [the longest x1 451 us: _layer_sums(): pl.pallas_call(functools.partial(_layer_kernel, m), out_shape=(jax.ShapeD...]
    psum x2 -> x0, waiting for transfers between devices: 481 us -> none  [the longest x1 259 us: layer(): p = lax.psum(_mm(o, wo).astype(jnp.bfloat16), 'tp')]
    dot_general x31 -> x0, matrix products: 327 us -> none  [the longest x7 232 us: _mm(): return jnp.dot(a, b, preferred_element_type=jnp.float32)]
    reduce_sum x14 -> x0, other arithmetic: 84 us -> none  [the longest x12 44.3 us: block(): pr = jax.nn.softmax(s, axis=-1).astype(jnp.bfloat16)]
    convert_element_type x17 -> x1, other arithmetic: 52.6 us -> 0.65 us  [layer(): ang = pos.astype(F32)[:, None] * inv[None, :]]
    gather x16 -> x0, local copies, waits for them, and re-layouts: 46.6 us -> none  [the longest x4 25.9 us: _cache(): jnp.take(k, (rows + l1) % t, axis=0)]
    dynamic_update_slice x12 -> x0, local copies, waits for them, and re-layouts: 11 us -> none  [_attend(): lax.map(block, (q.reshape(n // qb, qb, *q.shape[1:]), qrow.reshape(n // q...]
  transfers between devices with their start and end apart: 2 -> 0, of which waited for: 2 -> 0; matrix products, arithmetic and copies ran while one was open for 3% -> 0% of each run, Pallas kernels for 0% -> 0%
where the time goes in v1:
time: 662 us; the launch traced here: 661 us
  Pallas kernels  625 us (94%)
  local copies, waits for them, and re-layouts  24.5 us (4%)
  other arithmetic  10.6 us (2%)
    pallas_call x1, Pallas kernels, _layer_sums(): pl.pallas_call(functools.partial(_layer_kernel, m), out_shape=(jax.ShapeD...  451 us
    pallas_call x1, Pallas kernels, _attention(): pl.pallas_call(functools.partial(_attention_kernel, m), grid=(n // m,), o...  169 us
    unnamed x3, local copies, waits for them, and re-layouts  20.9 us

profile of v1, /device:TPU:81, one launch (start us, length us, event | category | flops | bytes accessed | tf_op | source)
XLA Modules:
  0.0 661.0 jit_solution(1217383073549733307)
XLA Ops:
  0.6 1.3 broadcast_in_dim.14.g_ref
  1.9 0.7 select_convert_fusion
  2.6 5.8 fusion
  8.4 2.5 pad_maximum_fusion.1
  11.0 1.7 constant_dynamic-slice_fusion
  12.7 1.6 pad_maximum_fusion.wkv_ref
  14.2 0.0 copy-start
  14.2 169.4 %attention.1 = (bf16[3072,512]{1,0:T(8,128)(2,1)}, bf16[3072,128]{1,0:T(8,128)(2,1)}, bf16[3072,128]{1,0:T(8,128)(2,1)}) custom-call(s32[2]{0:T(128)} %l1_ref.3, bf16[3072,4096]{1,0:T(8,128)(2,1)} %x_hbm.1, bf16[1,4096]{1,0:T(2,128)(2,1)} %broadcast_in_dim.14.g_ref, f32[3072,128]{1,0:T(8,128)} %get-tuple-element.21.cos_ref, ...), custom_call_target="tpu_custom_call" | custom-call | tf_op jit(solution)/shard_map/attention/pallas_call | solution.py:113
  183.6 0.0 copy-done
  183.6 0.6 broadcast_in_dim.15.g_ref
  184.2 450.8 %layer_sums.1 = (bf16[3072,4096]{1,0:T(8,128)(2,1)}, bf16[3072,4096]{1,0:T(8,128)(2,1)}) custom-call(bf16[3072,512]{1,0:T(8,128)(2,1)} %get-tuple-element.9.o_hbm, bf16[3072,4096]{1,0:T(8,128)(2,1)} %x_hbm.1, bf16[1,4096]{1,0:T(2,128)(2,1)} %broadcast_in_dim.15.g_ref, bf16[512,4096]{1,0:T(8,128)(2,1)} %wo_hbm.1, bf16[4096,1792]{1,0:T(8,128)(2,1)} %wg_hbm.1, ...), custom_call_target="tpu_custom_call" | custom-call | tf_op jit(solution)/shard_map/layer_sums/pallas_call | solution.py:444
  635.0 5.1 caches.1
  640.1 20.9 %copy.17 = bf16[3072,4096]{1,0:T(8,128)(2,1)} copy(bf16[3072,4096]{1,0:T(8,128)(2,1)} %get-tuple-element.28) | data formatting | bytes 50331648
  (1 shorter events, 0.0 us)
Async XLA Ops:
  14.2 169.4 %copy-start = (bf16[4096]{0:T(1024)(128)(2,1)S(1)}, bf16[4096]{0:T(1024)(128)(2,1)}, u32[]{:S(2)}) copy-start(bf16[4096]{0:T(1024)(128)(2,1)} %param.14) | copy-start | bytes 24580

commit v2 on v1

--- a/solution.py
+++ b/solution.py
@@ -92,38 +92,6 @@
         return 0
 
     lax.fori_loop(0, q_ref.shape[0], head, 0)
-
-
-def _attention_kernel(m, l1_ref, x_ref, g_ref, cos_ref, sin_ref, wq_ref, wkv_ref, o_ref, kc_ref, vc_ref,
-                      a_buf, q_buf, k_buf, v_buf, s_buf):
-    i = pl.program_id(0)
-    _norm_chunk(m, x_ref, g_ref[...].astype(F32), a_buf)
-    _project_chunk(i, m, a_buf, wq_ref, wkv_ref, cos_ref, sin_ref, q_buf, k_buf, v_buf)
-    kc_ref[...] = k_buf[_rows(i, m), :]
-    vc_ref[...] = v_buf[_rows(i, m), :]
-    _attend_chunk(i, m, l1_ref[0], q_buf, k_buf, v_buf, s_buf, o_ref)
-
-
-def _attention(x, lens, g1, cos, sin, wq, wkv):
-    n, d = x.shape
-    m = _rows_per_chunk(n)
-    hq = wq.shape[1]
-    full = lambda s: pl.BlockSpec(s, lambda i: (0, 0), pipeline_mode=pl.Buffered(buffer_count=1))
-    row = lambda c: pl.BlockSpec((m, c), lambda i: (i, 0))
-    return pl.pallas_call(
-        functools.partial(_attention_kernel, m),
-        grid=(n // m,),
-        out_shape=(jax.ShapeDtypeStruct((n, hq), BF16), jax.ShapeDtypeStruct((n, HEAD), BF16),
-                   jax.ShapeDtypeStruct((n, HEAD), BF16)),
-        in_specs=[pl.BlockSpec(memory_space=pltpu.SMEM), row(d), full((1, d)), row(HEAD), row(HEAD),
-                  full((d, hq)), full((d, 2 * HEAD))],
-        out_specs=(row(hq), row(HEAD), row(HEAD)),
-        scratch_shapes=[pltpu.VMEM((m, d), BF16), pltpu.VMEM((hq // HEAD, m, HEAD), BF16),
-                        pltpu.VMEM((n, HEAD), BF16), pltpu.VMEM((n, HEAD), BF16),
-                        pltpu.VMEM((n // m, m, m), F32)],
-        compiler_params=pltpu.CompilerParams(vmem_limit_bytes=VMEM_LIMIT, dimension_semantics=("arbitrary",)),
-        name="attention",
-    )(lens, x, g1, cos, sin, wq, wkv)
 
 
 class _Stream:
@@ -288,8 +256,10 @@
         self.keep(i).wait()
 
 
-def _layer_kernel(m, o_hbm, x_hbm, g_ref, wo_hbm, wg_hbm, wu_hbm, wd_hbm, y_hbm, b_hbm,
-                  wo_buf, o_buf, x_buf, h_buf, b_buf, u_buf, wgu_buf, wd_buf,
+def _layer_kernel(m, l1_ref, x_hbm, g1_ref, g2_ref, cos_hbm, sin_hbm, wq_hbm, wk_hbm, wv_hbm, wo_hbm, wg_hbm, wu_hbm, wd_hbm,
+                  y_hbm, b_hbm, k_hbm, v_hbm,
+                  wq_buf, wkv_buf, wo_buf, cos_buf, sin_buf, q_buf, k_buf, v_buf, s_buf, o_buf,
+                  x_buf, h_buf, xb_buf, u_buf, wgu_buf, wd_buf,
                   p_part, p_got, p_r1l, p_r1r, p_r2l, p_r2r, p_mine,
                   r_part, r_got, r_r1l, r_r1r, r_r2l, r_r2r, r_mine,
                   p_sems, r_sems, sems, wgu_sems, wd_sems):
@@ -305,7 +275,7 @@
         h_buf[i, a, :] = h
         hf = h.astype(F32)
         ms = jnp.mean(hf * hf, axis=-1, keepdims=True)
-        return (hf * lax.rsqrt(ms + EPS) * g_ref[...].astype(F32)).astype(BF16)
+        return (hf * lax.rsqrt(ms + EPS) * g2_ref[...].astype(F32)).astype(BF16)
 
     def finish_r(i, a, total):
         return (h_buf[i, a, :].astype(F32) + total.astype(F32)).astype(BF16)
@@ -326,18 +296,30 @@
     def wd(k, s):
         return pltpu.make_async_copy(wd_hbm.at[:, _cols(k, dt)], wd_buf.at[s], wd_sems.at[s])
 
-    def load_o(i):
-        return pltpu.make_async_copy(o_hbm.at[_rows(i, m), :], o_buf, sems.at[0])
+    def load_chunk(i):
+        r = _rows(i, m)
+        return (pltpu.make_async_copy(x_hbm.at[r, :], xb_buf, sems.at[0]),
+                pltpu.make_async_copy(cos_hbm.at[r, :], cos_buf, sems.at[4]),
+                pltpu.make_async_copy(sin_hbm.at[r, :], sin_buf, sems.at[5]))
+
+    def store_kv(i):
+        r = _rows(i, m)
+        return (pltpu.make_async_copy(k_buf.at[r, :], k_hbm.at[r, :], sems.at[6]),
+                pltpu.make_async_copy(v_buf.at[r, :], v_hbm.at[r, :], sems.at[7]))
 
     def load_x(i):
         return pltpu.make_async_copy(x_hbm.at[ps.place(i, ps.x), :], x_buf, sems.at[1])
 
     def load_b(i):
-        return pltpu.make_async_copy(b_hbm.at[_rows(i, m), :], b_buf, sems.at[2])
-
+        return pltpu.make_async_copy(b_hbm.at[_rows(i, m), :], xb_buf, sems.at[2])
+
+    head = _cols(lax.axis_index("tp"), HEAD)
     load_wo = pltpu.make_async_copy(wo_hbm, wo_buf, sems.at[3])
-    load_o(0).start()
-    load_wo.start()
+    load_qkv = (pltpu.make_async_copy(wk_hbm.at[:, head], wkv_buf.at[:, pl.ds(0, HEAD)], sems.at[8]),
+                pltpu.make_async_copy(wv_hbm.at[:, head], wkv_buf.at[:, pl.ds(HEAD, HEAD)], sems.at[9]),
+                pltpu.make_async_copy(wq_hbm, wq_buf, sems.at[10]))
+    for copy in (*load_chunk(0), *load_qkv, load_wo):
+        copy.start()
     for k in range(2):
         for copy in wgu(k % nf, k):
             copy.start()
@@ -349,7 +331,7 @@
             s = at % 2
             for copy in wgu(k, s):
                 copy.wait()
-            z = _dot(b_buf[...], wgu_buf[s])
+            z = _dot(xb_buf[...], wgu_buf[s])
             gate = z[:, :ft].astype(BF16).astype(F32)
             up = z[:, ft:].astype(BF16).astype(F32)
             u_buf[:, _cols(k, ft)] = (gate * (1.0 / (1.0 + jnp.exp(-gate))) * up).astype(BF16)
@@ -376,8 +358,22 @@
 
         lax.fori_loop(lo, hi, tile, 0)
 
-    def out_proj(i):
-        load_o(i).wait()
+    def project(i):
+        for copy in load_chunk(i):
+            copy.wait()
+        _norm_chunk(m, xb_buf, g1_ref[...].astype(F32), xb_buf)
+
+        @pl.when(i == 0)
+        def _():
+            for copy in load_qkv:
+                copy.wait()
+
+        _project_chunk(i, m, xb_buf, wq_buf, wkv_buf, cos_buf, sin_buf, q_buf, k_buf, v_buf)
+        for copy in store_kv(i):
+            copy.start()
+
+    def attend(i):
+        _attend_chunk(i, m, l1_ref[0], q_buf, k_buf, v_buf, s_buf, o_buf)
 
         @pl.when(i == 0)
         def _():
@@ -388,18 +384,17 @@
             return 0
 
         lax.fori_loop(0, nd, tile, 0)
-
-        @pl.when(i + 1 < nc)
-        def _():
-            load_o(i + 1).start()
+        for copy in store_kv(i):
+            copy.wait()
 
     def step(j, _):
         def at(delay):
             return lambda body: pl.when((j >= delay) & (j < nc + delay))(lambda: body(j - delay))
 
+        at(0)(project)
         at(4)(rs.s4)
         at(3)(rs.s1)
-        at(0)(out_proj)
+        at(0)(attend)
         at(1)(ps.s3)
         at(0)(ps.s0)
 
@@ -413,6 +408,12 @@
         at(4)(rs.s5)
         at(3)(rs.s2)
         at(2)(lambda i: gate_up(i, (nf + 1) // 2, nf))
+
+        @pl.when(j + 1 < nc)
+        def _():
+            for copy in load_chunk(j + 1):
+                copy.start()
+
         at(1)(ps.s4)
         at(0)(ps.s1)
         at(2)(lambda i: down(i, 0, nd // 2))
@@ -433,65 +434,89 @@
     lax.fori_loop(0, nc + 5, step, 0)
 
 
-def _layer_sums(o, x, g2, wo, wg, wu, wd):
+def _layer(x, lens, g1, g2, cos, sin, wq, wk, wv, wo, wg, wu, wd):
     n, d = x.shape
     m = _rows_per_chunk(n)
-    r, h, hq, f = m // 8, d // 2, o.shape[1], wg.shape[1]
+    r, h, hq, f = m // 8, d // 2, wq.shape[1], wg.shape[1]
     ft, dt = 256, 512
     stream = [pltpu.VMEM((m, d), BF16), pltpu.VMEM((2, 4 * r, d), BF16),
               pltpu.VMEM((2, r, d), BF16), pltpu.VMEM((2, r, d), BF16),
               pltpu.VMEM((2, r, h), BF16), pltpu.VMEM((2, r, h), BF16), pltpu.VMEM((2, r, d), BF16)]
+    whole, head = jax.ShapeDtypeStruct((n, d), BF16), jax.ShapeDtypeStruct((n, HEAD), BF16)
+    vmem = pl.BlockSpec(memory_space=pltpu.VMEM)
     return pl.pallas_call(
         functools.partial(_layer_kernel, m),
-        out_shape=(jax.ShapeDtypeStruct((n, d), BF16), jax.ShapeDtypeStruct((n, d), BF16)),
-        in_specs=[ANY, ANY, pl.BlockSpec(memory_space=pltpu.VMEM), ANY, ANY, ANY, ANY],
-        out_specs=(ANY, ANY),
+        out_shape=(whole, whole, head, head),
+        in_specs=[pl.BlockSpec(memory_space=pltpu.SMEM), ANY, vmem, vmem] + [ANY] * 9,
+        out_specs=(ANY,) * 4,
         scratch_shapes=[
-            pltpu.VMEM((hq, d), BF16), pltpu.VMEM((m, hq), BF16), pltpu.VMEM((r, d), BF16),
-            pltpu.VMEM((n // m, r, d), BF16), pltpu.VMEM((m, d), BF16), pltpu.VMEM((m, f), BF16),
-            pltpu.VMEM((2, d, 2 * ft), BF16), pltpu.VMEM((2, f, dt), BF16),
+            pltpu.VMEM((d, hq), BF16), pltpu.VMEM((d, 2 * HEAD), BF16), pltpu.VMEM((hq, d), BF16),
+            pltpu.VMEM((m, HEAD), F32), pltpu.VMEM((m, HEAD), F32), pltpu.VMEM((hq // HEAD, m, HEAD), BF16),
+            pltpu.VMEM((n, HEAD), BF16), pltpu.VMEM((n, HEAD), BF16), pltpu.VMEM((n // m, m, m), F32),
+            pltpu.VMEM((m, hq), BF16),
+            pltpu.VMEM((r, d), BF16), pltpu.VMEM((n // m, r, d), BF16), pltpu.VMEM((m, d), BF16),
+            pltpu.VMEM((m, f), BF16), pltpu.VMEM((2, d, 2 * ft), BF16), pltpu.VMEM((2, f, dt), BF16),
             *stream, *stream,
             pltpu.SemaphoreType.DMA((2, 2, 16)), pltpu.SemaphoreType.DMA((2, 2, 16)),
-            pltpu.SemaphoreType.DMA((4,)), pltpu.SemaphoreType.DMA((2, 2)), pltpu.SemaphoreType.DMA((2,)),
+            pltpu.SemaphoreType.DMA((11,)), pltpu.SemaphoreType.DMA((2, 2)), pltpu.SemaphoreType.DMA((2,)),
         ],
         compiler_params=pltpu.CompilerParams(collective_id=0, has_side_effects=True, vmem_limit_bytes=VMEM_LIMIT),
-        name="layer_sums",
-    )(o, x, g2, wo, wg, wu, wd)
-
-
-def _cache_kernel(m, l1_ref, k_ref, v_ref, ck_ref, cv_ref, k_buf, v_buf):
-    i = pl.program_id(0)
-    n = k_ref.shape[0]
+        name="layer",
+    )(lens, x, g1, g2, cos, sin, wq, wk, wv, wo, wg, wu, wd)
+
+
+def _finish_kernel(m, l1_ref, y_in, k_in, v_in, y_out, ck_out, cv_out, y_buf, k_buf, v_buf, kf_buf, vf_buf, ck_buf, cv_buf,
+                   in_sems, out_sems, sems):
+    n = y_in.shape[0]
+    nc = n // m
     l1 = l1_ref[0]
-
-    @pl.when(i == 0)
-    def _():
-        for src, buf in ((k_ref, k_buf), (v_ref, v_buf)):
-            buf[pl.ds(0, n), :] = src[...].astype(F32)
-            buf[pl.ds(n, m), :] = jnp.zeros((m, HEAD), F32)
-
-    rows = i * m + lax.broadcasted_iota(jnp.int32, (m, 1), 0)
-    start = jnp.minimum(l1 + i * m, n)
-    for buf, out in ((k_buf, ck_ref), (v_buf, cv_ref)):
-        out[0] = jnp.where(rows < l1, buf[_rows(i, m), :], 0.0).astype(BF16)
-        out[1] = jnp.where(rows < n - l1, buf[pl.ds(start, m), :], 0.0).astype(BF16)
-
-
-def _caches(lens, k, v):
-    n = k.shape[0]
+    rows = [pl.ds(i * m, m) for i in range(nc)]
+    loads = [pltpu.make_async_copy(y_in.at[rows[i], :], y_buf.at[i], in_sems.at[i]) for i in range(nc)]
+    stores = [pltpu.make_async_copy(y_buf.at[i], y_out.at[rows[i], :], out_sems.at[i]) for i in range(nc)]
+    heads = [pltpu.make_async_copy(k_in, k_buf, sems.at[0]), pltpu.make_async_copy(v_in, v_buf, sems.at[1])]
+    caches = [pltpu.make_async_copy(ck_buf, ck_out, sems.at[2]), pltpu.make_async_copy(cv_buf, cv_out, sems.at[3])]
+    for copy in heads + loads:
+        copy.start()
+    for copy in heads:
+        copy.wait()
+    for src, buf in ((k_buf, kf_buf), (v_buf, vf_buf)):
+        buf[pl.ds(n, m), :] = jnp.zeros((m, HEAD), F32)
+
+        def widen(i, _):
+            buf[_rows(i, m), :] = src[_rows(i, m), :].astype(F32)
+            return 0
+
+        lax.fori_loop(0, nc, widen, 0)
+    for i in range(nc):
+        loads[i].wait()
+        stores[i].start()
+        at = i * m + lax.broadcasted_iota(jnp.int32, (m, 1), 0)
+        start = jnp.minimum(l1 + i * m, n)
+        for buf, out in ((kf_buf, ck_buf), (vf_buf, cv_buf)):
+            out[0, rows[i], :] = jnp.where(at < l1, buf[rows[i], :], 0.0).astype(BF16)
+            out[1, rows[i], :] = jnp.where(at < n - l1, buf[pl.ds(start, m), :], 0.0).astype(BF16)
+    for copy in caches:
+        copy.start()
+    for copy in caches + stores:
+        copy.wait()
+
+
+def _finish(lens, y, k, v):
+    n, d = y.shape
     m = _rows_per_chunk(n)
-    whole = pl.BlockSpec((n, HEAD), lambda i: (0, 0))
-    out = pl.BlockSpec((2, m, HEAD), lambda i: (0, i, 0))
+    cache = jax.ShapeDtypeStruct((2, n, HEAD), BF16)
     return pl.pallas_call(
-        functools.partial(_cache_kernel, m),
-        grid=(n // m,),
-        out_shape=(jax.ShapeDtypeStruct((2, n, HEAD), BF16),) * 2,
-        in_specs=[pl.BlockSpec(memory_space=pltpu.SMEM), whole, whole],
-        out_specs=(out, out),
-        scratch_shapes=[pltpu.VMEM((n + m, HEAD), F32), pltpu.VMEM((n + m, HEAD), F32)],
-        compiler_params=pltpu.CompilerParams(dimension_semantics=("arbitrary",)),
-        name="caches",
-    )(lens, k, v)
+        functools.partial(_finish_kernel, m),
+        out_shape=(jax.ShapeDtypeStruct((n, d), BF16), cache, cache),
+        in_specs=[pl.BlockSpec(memory_space=pltpu.SMEM), ANY, ANY, ANY],
+        out_specs=(ANY,) * 3,
+        scratch_shapes=[pltpu.VMEM((n // m, m, d), BF16), pltpu.VMEM((n, HEAD), BF16), pltpu.VMEM((n, HEAD), BF16),
+                        pltpu.VMEM((n + m, HEAD), F32), pltpu.VMEM((n + m, HEAD), F32),
+                        pltpu.VMEM((2, n, HEAD), BF16), pltpu.VMEM((2, n, HEAD), BF16),
+                        pltpu.SemaphoreType.DMA((n // m,)), pltpu.SemaphoreType.DMA((n // m,)), pltpu.SemaphoreType.DMA((4,))],
+        compiler_params=pltpu.CompilerParams(vmem_limit_bytes=VMEM_LIMIT),
+        name="finish",
+    )(lens, y, k, v)
 
 
 def solution(mesh):
@@ -499,7 +524,6 @@
 
     def layer(x, lens, g1, g2, wq, wk, wv, wo, wg, wu, wd):
         n, d = x.shape
-        t = lax.axis_index("tp")
         l1 = lens[0]
         rows = jnp.arange(n)
         pos = jnp.where(rows >= l1, rows - l1, rows)
@@ -508,10 +532,8 @@
         c, s = jnp.cos(ang), jnp.sin(ang)
         cos = jnp.concatenate([c, c], axis=1)
         sin = jnp.concatenate([-s, s], axis=1)
-        wkv = jnp.concatenate([lax.dynamic_slice_in_dim(w, t * HEAD, HEAD, axis=1) for w in (wk, wv)], axis=1)
-        o, k, v = _attention(x, lens, g1[None], cos, sin, wq, wkv)
-        y, _ = _layer_sums(o, x, g2[None], wo, wg, wu, wd)
-        ck, cv = _caches(lens, k, v)
+        y, _, k, v = _layer(x, lens, g1[None], g2[None], cos, sin, wq, wk, wv, wo, wg, wu, wd)
+        y, ck, cv = _finish(lens, y, k, v)
         return y, ck[:, :, None, :], cv[:, :, None, :]
 
     row = P("dp", None)

time: 662 us -> 578 us (0.87)
  Pallas kernels: 625 us -> 564 us
  local copies, waits for them, and re-layouts: 24.5 us -> 2.62 us
    pallas_call x3 -> x2, Pallas kernels: 625 us -> 564 us  [the longest x1 546 us: _layer(): pl.pallas_call(functools.partial(_layer_kernel, m), out_shape=(whole, who...]
    unnamed x3 -> x0, local copies, waits for them, and re-layouts: 20.9 us -> none
where the time goes in v2:
time: 578 us; the launch traced here: 576 us
  Pallas kernels  564 us (98%)
  other arithmetic  8.98 us (2%)
    pallas_call x1, Pallas kernels, _layer(): pl.pallas_call(functools.partial(_layer_kernel, m), out_shape=(whole, who...  546 us
    pallas_call x1, Pallas kernels, _finish(): pl.pallas_call(functools.partial(_finish_kernel, m), out_shape=(jax.Shape...  18.2 us

profile of v2, /device:TPU:81, one launch (start us, length us, event | category | flops | bytes accessed | tf_op | source)
XLA Modules:
  0.0 576.4 jit_solution(611719479477743300)
XLA Ops:
  0.6 0.7 select_convert_fusion
  1.3 1.3 broadcast_in_dim.14.g1_ref
  2.6 1.3 broadcast_in_dim.15.g2_ref
  3.9 5.8 %fusion = (f32[3072,64]{1,0:T(8,128)S(1)}, f32[3072,64]{1,0:T(8,128)S(1)}, f32[3072,64]{1,0:T(8,128)S(1)}) fusion(f32[64]{0:T(128)S(1)} %multiply_power_fusion, f32[3072]{0:T(1024)S(1)} %select_convert_fusion), kind=kLoop, calls=%fused_computation.4 | loop fusion | flops 393216 | bytes 2371840 | tf_op jit(solution)/shard_map/neg | solution.py:534
  9.7 2.5 pad_maximum_fusion
  12.2 546.0 %layer.1 = (bf16[3072,4096]{1,0:T(8,128)(2,1)}, bf16[3072,4096]{1,0:T(8,128)(2,1)}, bf16[3072,128]{1,0:T(8,128)(2,1)}, bf16[3072,128]{1,0:T(8,128)(2,1)}) custom-call(s32[2]{0:T(128)} %l1_ref.3, bf16[3072,4096]{1,0:T(8,128)(2,1)} %x_hbm.1, bf16[1,4096]{1,0:T(2,128)(2,1)} %broadcast_in_dim.14.g1_ref, bf16[1,4096]{1,0:T(2,128)(2,1)} %broadcast_in_dim.15.g2_ref, ...), custom_call_target="tpu_custom_call" | custom-call | tf_op jit(solution)/shard_map/layer/pallas_call | solution.py:447
  558.2 18.2 %finish.1 = (bf16[3072,4096]{1,0:T(8,128)(2,1)}, bf16[2,3072,128]{2,1,0:T(8,128)(2,1)}, bf16[2,3072,128]{2,1,0:T(8,128)(2,1)}) custom-call(s32[2]{0:T(128)} %l1_ref.3, bf16[3072,4096]{1,0:T(8,128)(2,1)} %get-tuple-element.9.y_in, bf16[3072,128]{1,0:T(8,128)(2,1)} %get-tuple-element.10.k_in, bf16[3072,128]{1,0:T(8,128)(2,1)} %get-tuple-element.11.v_in), custom_call_target="tpu_custom_call" | custom-call | tf_op jit(solution)/shard_map/finish/pallas_call | solution.py:508
  (1 shorter events, 0.0 us)

commit v3 on v2

--- a/solution.py
+++ b/solution.py
@@ -33,65 +33,84 @@
 
 
 def _norm_chunk(m, x_ref, g, a_ref):
+    step = 32
+
     def body(k, _):
-        r = _rows(k, 16)
+        r = _rows(k, step)
         xf = x_ref[r, :].astype(F32)
         ms = jnp.mean(xf * xf, axis=-1, keepdims=True)
         a_ref[r, :] = (xf * lax.rsqrt(ms + EPS) * g).astype(BF16)
         return 0
 
-    lax.fori_loop(0, m // 16, body, 0)
-
-
-def _rope(z, cos, sin):
-    return z * cos + pltpu.roll(z, HEAD // 2, 1) * sin
-
-
-def _project_chunk(i, m, a_ref, wq_ref, wkv_ref, cos_ref, sin_ref, q_ref, k_ref, v_ref):
+    lax.fori_loop(0, m // step, body, 0)
+
+
+def _project_chunk(i, m, second, a_ref, wq_ref, wkv_ref, cos_ref, sin_ref, q_ref, k_ref, v_ref, vt_ref):
     a = a_ref[...]
+    low = lax.broadcasted_iota(jnp.int32, (m, HEAD), 1) < HEAD // 2
+    mine = low != (second > 0)
     cos, sin = cos_ref[...], sin_ref[...]
+    cos = jnp.where(mine, cos, pltpu.roll(cos, HEAD // 2, 1))
+    sin = jnp.where(mine, sin, pltpu.roll(sin, HEAD // 2, 1))
+    sin = jnp.where(low, -sin, sin)
+
+    def rope(z):
+        return (z * cos + pltpu.roll(z, HEAD // 2, 1) * sin).astype(BF16)
+
     kv = _dot(a, wkv_ref[...])
-    r = _rows(i, m)
-    k_ref[r, :] = _rope(kv[:, :HEAD], cos, sin).astype(BF16)
-    v_ref[r, :] = kv[:, HEAD:].astype(BF16)
+    k_ref[_rows(i, m), :] = rope(kv[:, :HEAD])
+    v = kv[:, HEAD:]
+    v_ref[...] = v.astype(BF16)
+    vt_ref[:, _cols(i, m)] = v.T.astype(BF16)
     q = _dot(a, wq_ref[...])
-    for h in range(q_ref.shape[0]):
-        q_ref[h] = _rope(q[:, h * HEAD:(h + 1) * HEAD], cos, sin).astype(BF16)
-
-
-def _attend_chunk(i, m, l1, q_ref, k_ref, v_ref, s_ref, o_ref):
-    rows = i * m + lax.broadcasted_iota(jnp.int32, (m, 1), 0)
+    for h in range(q.shape[1] // HEAD):
+        q_ref[pl.ds(h * m, m), :] = rope(q[:, h * HEAD:(h + 1) * HEAD])
+
+
+def _attend_heads(i, m, l1, h0, heads, q_ref, k_ref, vt_ref, s_ref, acc_ref, o_ref):
+    w = heads * m
+    q = q_ref[pl.ds(h0 * m, w), :]
+    rows = lax.broadcasted_iota(jnp.int32, (1, w), 1)
+    for _ in range(heads - 1):
+        rows = jnp.where(rows >= m, rows - m, rows)
+    rows = rows + i * m
     first = jnp.where(rows >= l1, l1, 0)
     scale = HEAD ** -0.5 * 1.4426950408889634
 
-    def head(h, _):
-        q = q_ref[h]
-
-        def score(b, top):
-            s = lax.dot_general(q, k_ref[_rows(b, m), :], (((1,), (1,)), ((), ())), preferred_element_type=F32)
-            cols = b * m + lax.broadcasted_iota(jnp.int32, (1, m), 1)
-            s = jnp.where((cols <= rows) & (cols >= first), s, -jnp.inf)
-            s_ref[b] = s
-            return jnp.maximum(top, jnp.max(s, axis=1, keepdims=True))
-
-        top = lax.fori_loop(0, i + 1, score, jnp.full((m, 1), -jnp.inf, F32))
-
-        def expo(b, total):
-            e = jnp.exp2((s_ref[b] - top) * scale)
-            s_ref[b] = e
-            return total + jnp.sum(e, axis=1, keepdims=True)
-
-        total = lax.fori_loop(0, i + 1, expo, jnp.zeros((m, 1), F32))
-        inv = 1.0 / total
-
-        def value(b, acc):
-            return acc + _dot((s_ref[b] * inv).astype(BF16), v_ref[_rows(b, m), :])
-
-        acc = lax.fori_loop(0, i + 1, value, jnp.zeros((m, HEAD), F32))
-        o_ref[:, _cols(h, HEAD)] = acc.astype(BF16)
-        return 0
-
-    lax.fori_loop(0, q_ref.shape[0], head, 0)
+    def scores(b):
+        return lax.dot_general(k_ref[_rows(b, m), :], q, (((1,), (1,)), ((), ())), preferred_element_type=F32)
+
+    def keys(b):
+        return b * m + lax.broadcasted_iota(jnp.int32, (m, 1), 0)
+
+    def take(b, top, total, new):
+        peak = jnp.maximum(top, new)
+        alpha = jnp.exp2((top - peak) * scale)
+        e = jnp.exp2((s_ref[...] - peak) * scale)
+        total = total * alpha + jnp.sum(e, axis=0, keepdims=True)
+        acc_ref[...] = acc_ref[...] * alpha + _dot(vt_ref[:, _cols(b, m)], e.astype(BF16))
+        return peak, total
+
+    def put(s):
+        s_ref[...] = s
+        return jnp.max(s, axis=0, keepdims=True)
+
+    acc_ref[...] = jnp.zeros_like(acc_ref)
+    s = scores(i)
+    new = put(jnp.where((keys(i) <= rows) & (keys(i) >= first), s, -jnp.inf))
+    top, total = jnp.full((1, w), -jnp.inf, F32), jnp.zeros((1, w), F32)
+
+    def block(b, carry):
+        top, total, new = carry
+        s = scores(b)
+        top, total = take(jnp.where(b == 0, i, b - 1), top, total, new)
+        return top, total, put(jnp.where(keys(b) >= first, s, -jnp.inf))
+
+    top, total, new = lax.fori_loop(0, i, block, (top, total, new))
+    top, total = take(jnp.where(i == 0, i, i - 1), top, total, new)
+    o = acc_ref[...] * (1.0 / total)
+    for h in range(heads):
+        o_ref[:, pl.ds((h0 + h) * HEAD, HEAD)] = o[:, h * m:(h + 1) * m].T.astype(BF16)
 
 
 class _Stream:
@@ -258,15 +277,16 @@
 
 def _layer_kernel(m, l1_ref, x_hbm, g1_ref, g2_ref, cos_hbm, sin_hbm, wq_hbm, wk_hbm, wv_hbm, wo_hbm, wg_hbm, wu_hbm, wd_hbm,
                   y_hbm, b_hbm, k_hbm, v_hbm,
-                  wq_buf, wkv_buf, wo_buf, cos_buf, sin_buf, q_buf, k_buf, v_buf, s_buf, o_buf,
+                  wq_buf, wkv_buf, wo_buf, cos_buf, sin_buf, q_buf, k_buf, v_buf, vt_buf, s_buf, acc_buf, o_buf,
                   x_buf, h_buf, xb_buf, u_buf, wgu_buf, wd_buf,
-                  p_part, p_got, p_r1l, p_r1r, p_r2l, p_r2r, p_mine,
-                  r_part, r_got, r_r1l, r_r1r, r_r2l, r_r2r, r_mine,
+                  part, p_got, p_r1l, p_r1r, p_r2l, p_r2r, p_mine,
+                  r_got, r_r1l, r_r1r, r_r2l, r_r2r, r_mine,
                   p_sems, r_sems, sems, wgu_sems, wd_sems):
     n, d = x_hbm.shape
     f = wg_hbm.shape[1]
     ft, dt = wgu_buf.shape[2] // 2, wd_buf.shape[2]
     nf, nd, nc = f // ft, d // dt, n // m
+    ot = 1024
     r = m // 8
 
     def finish_p(i, a, total):
@@ -275,13 +295,13 @@
         h_buf[i, a, :] = h
         hf = h.astype(F32)
         ms = jnp.mean(hf * hf, axis=-1, keepdims=True)
-        return (hf * lax.rsqrt(ms + EPS) * g2_ref[...].astype(F32)).astype(BF16)
+        return (hf * lax.rsqrt(ms + EPS) * g2_ref[...].astype(F32)[None]).astype(BF16)
 
     def finish_r(i, a, total):
         return (h_buf[i, a, :].astype(F32) + total.astype(F32)).astype(BF16)
 
-    ps = _Stream(m, p_part, p_got, p_r1l, p_r1r, p_r2l, p_r2r, p_mine, b_hbm, p_sems, finish_p)
-    rs = _Stream(m, r_part, r_got, r_r1l, r_r1r, r_r2l, r_r2r, r_mine, y_hbm, r_sems, finish_r)
+    ps = _Stream(m, part, p_got, p_r1l, p_r1r, p_r2l, p_r2r, p_mine, b_hbm, p_sems, finish_p)
+    rs = _Stream(m, part, r_got, r_r1l, r_r1r, r_r2l, r_r2r, r_mine, y_hbm, r_sems, finish_r)
 
     barrier = pltpu.get_barrier_semaphore()
     for to in (ps.right, ps.left, ps.twin):
@@ -298,14 +318,15 @@
 
     def load_chunk(i):
         r = _rows(i, m)
+        t = _rows(i % (nc // 2), m)
         return (pltpu.make_async_copy(x_hbm.at[r, :], xb_buf, sems.at[0]),
-                pltpu.make_async_copy(cos_hbm.at[r, :], cos_buf, sems.at[4]),
-                pltpu.make_async_copy(sin_hbm.at[r, :], sin_buf, sems.at[5]))
+                pltpu.make_async_copy(cos_hbm.at[t, :], cos_buf, sems.at[4]),
+                pltpu.make_async_copy(sin_hbm.at[t, :], sin_buf, sems.at[5]))
 
     def store_kv(i):
         r = _rows(i, m)
         return (pltpu.make_async_copy(k_buf.at[r, :], k_hbm.at[r, :], sems.at[6]),
-                pltpu.make_async_copy(v_buf.at[r, :], v_hbm.at[r, :], sems.at[7]))
+                pltpu.make_async_copy(v_buf, v_hbm.at[r, :], sems.at[7]))
 
     def load_x(i):
         return pltpu.make_async_copy(x_hbm.at[ps.place(i, ps.x), :], x_buf, sems.at[1])
@@ -313,17 +334,14 @@
     def load_b(i):
         return pltpu.make_async_copy(b_hbm.at[_rows(i, m), :], xb_buf, sems.at[2])
 
+    heads = wq_hbm.shape[1] // HEAD
     head = _cols(lax.axis_index("tp"), HEAD)
     load_wo = pltpu.make_async_copy(wo_hbm, wo_buf, sems.at[3])
     load_qkv = (pltpu.make_async_copy(wk_hbm.at[:, head], wkv_buf.at[:, pl.ds(0, HEAD)], sems.at[8]),
                 pltpu.make_async_copy(wv_hbm.at[:, head], wkv_buf.at[:, pl.ds(HEAD, HEAD)], sems.at[9]),
                 pltpu.make_async_copy(wq_hbm, wq_buf, sems.at[10]))
-    for copy in (*load_chunk(0), *load_qkv, load_wo):
+    for copy in (*load_chunk(0), *load_qkv):
         copy.start()
-    for k in range(2):
-        for copy in wgu(k % nf, k):
-            copy.start()
-        wd(k % nd, k).start()
 
     def gate_up(i, lo, hi):
         def tile(k, _):
@@ -349,7 +367,7 @@
             at = i * nd + k
             s = at % 2
             wd(k, s).wait()
-            r_part[:, _cols(k, dt)] = _dot(u_buf[...], wd_buf[s]).astype(BF16)
+            part[:, _cols(k, dt)] = _dot(u_buf[...], wd_buf[s]).astype(BF16)
 
             @pl.when(at + 2 < nc * nd)
             def _():
@@ -361,29 +379,35 @@
     def project(i):
         for copy in load_chunk(i):
             copy.wait()
-        _norm_chunk(m, xb_buf, g1_ref[...].astype(F32), xb_buf)
+        _norm_chunk(m, xb_buf, g1_ref[...].astype(F32)[None], xb_buf)
 
         @pl.when(i == 0)
         def _():
             for copy in load_qkv:
                 copy.wait()
-
-        _project_chunk(i, m, xb_buf, wq_buf, wkv_buf, cos_buf, sin_buf, q_buf, k_buf, v_buf)
+            load_wo.start()
+            for k in range(2):
+                for copy in wgu(k % nf, k):
+                    copy.start()
+                wd(k % nd, k).start()
+
+        _project_chunk(i, m, i // (nc // 2), xb_buf, wq_buf, wkv_buf, cos_buf, sin_buf, q_buf, k_buf, v_buf, vt_buf)
         for copy in store_kv(i):
             copy.start()
 
     def attend(i):
-        _attend_chunk(i, m, l1_ref[0], q_buf, k_buf, v_buf, s_buf, o_buf)
+        for h in range(0, heads, 2):
+            _attend_heads(i, m, l1_ref[0], h, 2, q_buf, k_buf, vt_buf, s_buf, acc_buf, o_buf)
 
         @pl.when(i == 0)
         def _():
             load_wo.wait()
 
         def tile(k, _):
-            p_part[:, _cols(k, dt)] = _dot(o_buf[...], wo_buf[:, _cols(k, dt)]).astype(BF16)
-            return 0
-
-        lax.fori_loop(0, nd, tile, 0)
+            part[:, _cols(k, ot)] = _dot(o_buf[...], wo_buf[:, _cols(k, ot)]).astype(BF16)
+            return 0
+
+        lax.fori_loop(0, d // ot, tile, 0)
         for copy in store_kv(i):
             copy.wait()
 
@@ -439,7 +463,7 @@
     m = _rows_per_chunk(n)
     r, h, hq, f = m // 8, d // 2, wq.shape[1], wg.shape[1]
     ft, dt = 256, 512
-    stream = [pltpu.VMEM((m, d), BF16), pltpu.VMEM((2, 4 * r, d), BF16),
+    stream = [pltpu.VMEM((2, 4 * r, d), BF16),
               pltpu.VMEM((2, r, d), BF16), pltpu.VMEM((2, r, d), BF16),
               pltpu.VMEM((2, r, h), BF16), pltpu.VMEM((2, r, h), BF16), pltpu.VMEM((2, r, d), BF16)]
     whole, head = jax.ShapeDtypeStruct((n, d), BF16), jax.ShapeDtypeStruct((n, HEAD), BF16)
@@ -451,12 +475,12 @@
         out_specs=(ANY,) * 4,
         scratch_shapes=[
             pltpu.VMEM((d, hq), BF16), pltpu.VMEM((d, 2 * HEAD), BF16), pltpu.VMEM((hq, d), BF16),
-            pltpu.VMEM((m, HEAD), F32), pltpu.VMEM((m, HEAD), F32), pltpu.VMEM((hq // HEAD, m, HEAD), BF16),
-            pltpu.VMEM((n, HEAD), BF16), pltpu.VMEM((n, HEAD), BF16), pltpu.VMEM((n // m, m, m), F32),
-            pltpu.VMEM((m, hq), BF16),
+            pltpu.VMEM((m, HEAD), F32), pltpu.VMEM((m, HEAD), F32), pltpu.VMEM((hq // HEAD * m, HEAD), BF16),
+            pltpu.VMEM((n, HEAD), BF16), pltpu.VMEM((m, HEAD), BF16), pltpu.VMEM((HEAD, n), BF16),
+            pltpu.VMEM((m, 2 * m), F32), pltpu.VMEM((HEAD, 2 * m), F32), pltpu.VMEM((m, hq), BF16),
             pltpu.VMEM((r, d), BF16), pltpu.VMEM((n // m, r, d), BF16), pltpu.VMEM((m, d), BF16),
             pltpu.VMEM((m, f), BF16), pltpu.VMEM((2, d, 2 * ft), BF16), pltpu.VMEM((2, f, dt), BF16),
-            *stream, *stream,
+            pltpu.VMEM((m, d), BF16), *stream, *stream,
             pltpu.SemaphoreType.DMA((2, 2, 16)), pltpu.SemaphoreType.DMA((2, 2, 16)),
             pltpu.SemaphoreType.DMA((11,)), pltpu.SemaphoreType.DMA((2, 2)), pltpu.SemaphoreType.DMA((2,)),
         ],
@@ -528,11 +552,10 @@
         rows = jnp.arange(n)
         pos = jnp.where(rows >= l1, rows - l1, rows)
         inv = BASE ** (-jnp.arange(0, HEAD, 2, dtype=F32) / HEAD)
-        ang = pos.astype(F32)[:, None] * inv[None, :]
-        c, s = jnp.cos(ang), jnp.sin(ang)
-        cos = jnp.concatenate([c, c], axis=1)
-        sin = jnp.concatenate([-s, s], axis=1)
-        y, _, k, v = _layer(x, lens, g1[None], g2[None], cos, sin, wq, wk, wv, wo, wg, wu, wd)
+        pos = pos.astype(F32).reshape(2, n // 2, 1)
+        ang = jnp.where(jnp.arange(HEAD) < HEAD // 2, pos[0], pos[1]) * jnp.concatenate([inv, inv])
+        cos, sin = jnp.cos(ang), jnp.sin(ang)
+        y, _, k, v = _layer(x, lens, g1, g2, cos, sin, wq, wk, wv, wo, wg, wu, wd)
         y, ck, cv = _finish(lens, y, k, v)
         return y, ck[:, :, None, :], cv[:, :, None, :]
 

time: 578 us -> 490 us (0.85)
  Pallas kernels: 564 us -> 484 us
    pallas_call x1, Pallas kernels: 546 us -> 465 us  [_layer(): pl.pallas_call(functools.partial(_layer_kernel, m), out_shape=(whole, who...]
where the time goes in v3:
time: 490 us; the launch traced here: 489 us
  Pallas kernels  484 us (99%)
  other arithmetic  5.08 us (1%)
    pallas_call x1, Pallas kernels, _layer(): pl.pallas_call(functools.partial(_layer_kernel, m), out_shape=(whole, who...  465 us
    pallas_call x1, Pallas kernels, _finish(): pl.pallas_call(functools.partial(_finish_kernel, m), out_shape=(jax.Shape...  18.2 us

profile of v3, /device:TPU:81, one launch (start us, length us, event | category | flops | bytes accessed | tf_op | source)
XLA Modules:
  0.0 489.4 jit_solution(12917015450929342666)
XLA Ops:
  0.7 0.1 pad_maximum_fusion
  0.7 0.7 select_convert_fusion
  1.4 4.3 fusion
  5.7 465.4 %layer.1 = (bf16[3072,4096]{1,0:T(8,128)(2,1)}, bf16[3072,4096]{1,0:T(8,128)(2,1)}, bf16[3072,128]{1,0:T(8,128)(2,1)}, bf16[3072,128]{1,0:T(8,128)(2,1)}) custom-call(s32[2]{0:T(128)} %l1_ref.3, bf16[3072,4096]{1,0:T(8,128)(2,1)} %x_hbm.1, bf16[4096]{0:T(1024)(128)(2,1)} %g1_ref.1, bf16[4096]{0:T(1024)(128)(2,1)} %g2_ref.1, ...), custom_call_target="tpu_custom_call" | custom-call | tf_op jit(solution)/shard_map/layer/pallas_call | solution.py:471
  471.2 18.2 %finish.1 = (bf16[3072,4096]{1,0:T(8,128)(2,1)}, bf16[2,3072,128]{2,1,0:T(8,128)(2,1)}, bf16[2,3072,128]{2,1,0:T(8,128)(2,1)}) custom-call(s32[2]{0:T(128)} %l1_ref.3, bf16[3072,4096]{1,0:T(8,128)(2,1)} %get-tuple-element.9.y_in, bf16[3072,128]{1,0:T(8,128)(2,1)} %get-tuple-element.10.k_in, bf16[3072,128]{1,0:T(8,128)(2,1)} %get-tuple-element.11.v_in), custom_call_target="tpu_custom_call" | custom-call | tf_op jit(solution)/shard_map/finish/pallas_call | solution.py:532
  (3 shorter events, 0.0 us)
